TPU v7x, 32 devices: a whole 2x2x4 slice. The times are simulated.
32 devices in a mesh: wall: 4 (over z), span: 8 (over y, x, core).
Axes of the slice: x: 2, y: 2, z: 4, core: 2. Of those that a mesh axis runs over, the one named last changes fastest.
Arguments:
- noise_bits: int32 [3, 32, 512, 1024], P(None, None, 'span', 'wall'), may hold values from 0 to 1073741823
- filter_widths: int32 [1024], P('wall'), may hold values from 8 to 64, as said below
- target_mean_profile: float32 [3, 1024], P(None, 'wall'), may hold values from -4 to 4
- target_factor_diagonal: float32 [3, 1024], P(None, 'wall'), may hold values from 0.3 to 2
- target_factor_lower: float32 [3, 1024], P(None, 'wall'), may hold values from -0.8 to 0.8
Outputs:
- inflow_field: float32 [3, 32, 512, 1024], P(None, None, 'span', 'wall')
Inputs may be any that keep to these rules, and one draw needn't show every extreme that they name: `filter_widths`: every row's width lies between 8 and 64, and both ends occur in every draw.
All inputs are finite; a program needn't handle non-finite values.
Results may differ from a plain program's by a relative error of at most 0.0045.
Values may be sent and summed in bfloat16 or wider, within the bound.
A program may use at most 64 MiB of HBM per device.

v0:
```python
import math

import jax
import jax.numpy as jnp
from jax import lax
from jax.sharding import PartitionSpec as P

WMAX = 64
SPANW = 32
TSCALE = 8


PAIRS = ((0, 0), (1, 0), (1, 1), (2, 0), (2, 1), (2, 2))
SPREAD_FLOOR = 0.25
INV_RANGE = 1.0 / 1073741824.0


def padded_2(cells, sides, width, closed):
    for axis, dim in sides:
        count = lax.axis_size(axis)
        ends = count if closed else count - 1
        head = lax.slice_in_dim(cells, 0, width, axis=dim)
        tail = lax.slice_in_dim(cells, cells.shape[dim] - width, cells.shape[dim], axis=dim)
        cells = jnp.concatenate(
            [
                lax.ppermute(tail, axis, [(i, (i + 1) % count) for i in range(ends)]),
                cells,
                lax.ppermute(head, axis, [((i + 1) % count, i) for i in range(ends)]),
            ],
            axis=dim,
        )
    return cells


def to_field(noise_bits):
    scaled = (noise_bits.astype(jnp.float32) + 0.5) * INV_RANGE - 0.5
    return (math.sqrt(12.0) * scaled).astype(jnp.bfloat16)


def band_matrix(cell_widths, in_count, margin):
    out_count = cell_widths.shape[0]
    offsets = (
        lax.broadcasted_iota(jnp.int32, (out_count, in_count), 1)
        - margin
        - lax.broadcasted_iota(jnp.int32, (out_count, in_count), 0)
    ).astype(jnp.float32)
    spread = cell_widths[:, None]
    inside = jnp.abs(offsets) <= 2.0 * spread
    safe_off = jnp.where(inside, offsets, 0.0)
    kernel = jnp.where(
        inside, jnp.exp(-math.pi * safe_off * safe_off / (8.0 * spread * spread)), 0.0
    )
    norm_total = jnp.sqrt(jnp.sum(kernel * kernel, axis=1, keepdims=True))
    return (kernel / norm_total).astype(jnp.bfloat16)


def time_matrix(sample_count):
    later_idx = lax.broadcasted_iota(jnp.int32, (sample_count, sample_count), 0)
    earlier = lax.broadcasted_iota(jnp.int32, (sample_count, sample_count), 1)
    causal = later_idx >= earlier
    lagged = jnp.where(causal, later_idx - earlier, 0).astype(jnp.float32)
    decay_rate = math.exp(-math.pi / (2.0 * TSCALE))
    fresh_gain = jnp.where(earlier == 0, 1.0, math.sqrt(1.0 - decay_rate * decay_rate))
    return jnp.where(causal, jnp.exp(-math.pi * lagged / (2.0 * TSCALE)) * fresh_gain, 0.0)


def lund_transform(sample_covariance, target_factor_diagonal, target_factor_lower):
    cov_00 = sample_covariance[0] + SPREAD_FLOOR
    cov_10 = sample_covariance[1]
    cov_11 = sample_covariance[2] + SPREAD_FLOOR
    cov_20 = sample_covariance[3]
    cov_21 = sample_covariance[4]
    cov_22 = sample_covariance[5] + SPREAD_FLOOR
    chol_00 = jnp.sqrt(cov_00)
    chol_10 = cov_10 / chol_00
    chol_20 = cov_20 / chol_00
    chol_11 = jnp.sqrt(cov_11 - chol_10 * chol_10)
    chol_21 = (cov_21 - chol_20 * chol_10) / chol_11
    chol_22 = jnp.sqrt(cov_22 - chol_20 * chol_20 - chol_21 * chol_21)
    inv_00 = 1.0 / chol_00
    inv_11 = 1.0 / chol_11
    inv_22 = 1.0 / chol_22
    inv_10 = -chol_10 * inv_00 * inv_11
    inv_21 = -chol_21 * inv_11 * inv_22
    inv_20 = -(chol_20 * inv_00 + chol_21 * inv_10) * inv_22
    gain_00 = target_factor_diagonal[0] * inv_00
    gain_10 = target_factor_lower[0] * inv_00 + target_factor_diagonal[1] * inv_10
    gain_11 = target_factor_diagonal[1] * inv_11
    gain_20 = (
        target_factor_lower[1] * inv_00
        + target_factor_lower[2] * inv_10
        + target_factor_diagonal[2] * inv_20
    )
    gain_21 = target_factor_lower[2] * inv_11 + target_factor_diagonal[2] * inv_21
    gain_22 = target_factor_diagonal[2] * inv_22
    return jnp.stack([gain_00, gain_10, gain_11, gain_20, gain_21, gain_22])


def rescaled_inflow(fluctuation, per_row_means, scaling_terms, velocity_profile):
    centred_samples = fluctuation - per_row_means[:, None, None, :]
    first_component = velocity_profile[0] + scaling_terms[0] * centred_samples[0]
    second_component = (
        velocity_profile[1]
        + scaling_terms[1] * centred_samples[0]
        + scaling_terms[2] * centred_samples[1]
    )
    third_component = (
        velocity_profile[2]
        + scaling_terms[3] * centred_samples[0]
        + scaling_terms[4] * centred_samples[1]
        + scaling_terms[5] * centred_samples[2]
    )
    return jnp.stack([first_component, second_component, third_component])


def pair_sums(values):
    return jnp.stack(
        [jnp.sum(values[first_c] * values[second_c], axis=(0, 1)) for first_c, second_c in PAIRS]
    )


def raw_spread(moments, per_row_means):
    return jnp.stack(
        [
            moments[slot] - per_row_means[first_c] * per_row_means[second_c]
            for slot, (first_c, second_c) in enumerate(PAIRS)
        ]
    )


def span_filter(widened, span_band):
    return jnp.einsum("kj,csjy->csky", span_band, widened, preferred_element_type=jnp.float32)


def time_filter(spanned, memory):
    return jnp.einsum("ts,csky->ctky", memory, spanned, precision=lax.Precision.HIGHEST)


def shards(
    noise_bits, filter_widths, target_mean_profile, target_factor_diagonal, target_factor_lower
):
    n_comp, n_samples, n_cols, n_rows = noise_bits.shape
    span_count = lax.axis_size("span")
    margin = 2 * WMAX
    span_margin = 2 * SPANW
    psi_field = to_field(noise_bits)
    padded = padded_2(psi_field, (("wall", 3),), margin, False)
    wall_band = band_matrix(filter_widths.astype(jnp.float32), n_rows + 2 * margin, margin)
    smooth = jnp.einsum(
        "csjm,ym->csjy", padded, wall_band, preferred_element_type=jnp.float32
    ).astype(jnp.bfloat16)
    span_band = band_matrix(
        jnp.full((n_cols,), float(SPANW), jnp.float32), n_cols + 2 * span_margin, span_margin
    )
    memory = time_matrix(n_samples)
    cell_count = float(n_samples * n_cols * span_count)
    widened = padded_2(smooth, (("span", 2),), span_margin, True)
    fluctuation = time_filter(span_filter(widened, span_band), memory)
    local_sums = jnp.sum(fluctuation, axis=(1, 2))
    total_sums, total_pairs = lax.psum((local_sums, pair_sums(fluctuation)), "span")
    per_row_means = total_sums / cell_count
    sample_covariance = raw_spread(total_pairs / cell_count, per_row_means)
    scaling_terms = lund_transform(sample_covariance, target_factor_diagonal, target_factor_lower)
    return rescaled_inflow(fluctuation, per_row_means, scaling_terms, target_mean_profile)


def solution(mesh):
    placed = (
        P(None, None, "span", "wall"),
        P("wall"),
        P(None, "wall"),
        P(None, "wall"),
        P(None, "wall"),
    )
    return jax.shard_map(
        shards, mesh=mesh, in_specs=placed, out_specs=P(None, None, "span", "wall"), check_vma=False
    )
```

profile of v0, /device:TPU:0, one launch (start us, length us, event | category | flops | bytes accessed | tf_op | source)
XLA Modules:
  0.0 171.7 jit_solution(5421525174298413264)
XLA Ops:
  0.0 3.9 %multiply_convert_fusion = bf16[3,32,64,256]{3,2,1,0:T(8,128)(2,1)S(1)} fusion(s32[3,32,64,256]{3,2,1,0:T(8,128)} %param.5), kind=kLoop, calls=%fused_computation.16 | loop fusion | flops 9437184 | bytes 9437184 | tf_op jit(solution)/shard_map/convert_element_type | solution.py:37
  3.9 0.0 copy-start.4
  4.0 0.9 fusion.66
  4.9 5.1 %collective-permute-start = (bf16[3,32,64,128]{3,2,1,0:T(8,128)(2,1)S(1)}, bf16[3,32,64,128]{3,2,1,0:T(8,128)(2,1)S(1)}, u32[]{:S(2)}, u32[]{:S(2)}) collective-permute-start(bf16[3,32,64,128]{3,2,1,0:T(8,128)(2,1)S(1)} %get-tuple-element.20), channel_id=1, source_target_pairs={{0,8},{8,16},{16,24},{1,9},{9,17},{17,25},{2,10},{10,18},{18,26},{... | collective-permute-start | bytes 4718600 | tf_op jit(solution)/shard_map/ppermute | solution.py:26
  10.0 1.3 collective-permute-start.1
  11.3 0.0 copy-done.4
  11.3 0.4 multiply_reduce_fusion.6
  11.7 0.0 copy-start.1
  11.7 0.0 copy-start.2
  11.7 31.8 %collective-permute-done = bf16[3,32,64,128]{3,2,1,0:T(8,128)(2,1)S(1)} collective-permute-done((bf16[3,32,64,128]{3,2,1,0:T(8,128)(2,1)S(1)}, bf16[3,32,64,128]{3,2,1,0:T(8,128)(2,1)S(1)}, u32[]{:S(2)}, u32[]{:S(2)}) %collective-permute-start) | collective-permute-done | bytes 1572896 | tf_op jit(solution)/shard_map/ppermute | solution.py:26
  43.5 4.2 %collective-permute-done.1 = bf16[3,32,64,128]{3,2,1,0:T(8,128)(2,1)S(1)} collective-permute-done((bf16[3,32,64,128]{3,2,1,0:T(8,128)(2,1)S(1)}, bf16[3,32,64,128]{3,2,1,0:T(8,128)(2,1)S(1)}, u32[]{:S(2)}, u32[]{:S(2)}) %collective-permute-start.1) | collective-permute-done | bytes 1572896 | tf_op jit(solution)/shard_map/ppermute | solution.py:28
  47.7 2.5 %fusion.18 = bf16[3,32,64,256]{3,2,1,0:T(8,128)(2,1)S(1)} fusion(bf16[3,32,64,128]{3,2,1,0:T(8,128)(2,1)S(1)} %collective-permute-done.1, bf16[3,32,64,256]{3,2,1,0:T(8,128)(2,1)S(1)} %multiply_convert_fusion, bf16[3,32,64,128]{3,2,1,0:T(8,128)(2,1)S(1)} %collective-permute-done, f32[256]{0:T(256)S(1)} %sqrt.63, f32[256]{0:T(256)S(1)} %get-tuple-element.44, ...), kind=kOutput, calls=%fused_computation.19 | convolution fusion | flops 1632501760 | bytes 9442304 | tf_op jit(solution)/shard_map/csjm,ym->csjy/dot_general | solution.py:149
  50.2 0.1 collective-permute-start.2
  50.3 2.6 %collective-permute-start.3 = (bf16[3,32,64,256]{3,2,1,0:T(8,128)(2,1)S(1)}, bf16[3,32,64,256]{3,2,1,0:T(8,128)(2,1)S(1)}, u32[]{:S(2)}, u32[]{:S(2)}) collective-permute-start(bf16[3,32,64,256]{3,2,1,0:T(8,128)(2,1)S(1)} %fusion.18), channel_id=1, source_target_pairs={{1,0},{2,1},{3,2},{4,3},{5,4},{6,5},{7,6},{0,7},{9,8},{10,9},{11,1... | collective-permute-start | bytes 9437192 | tf_op jit(solution)/shard_map/ppermute | solution.py:28
  52.9 0.1 multiply_reduce_fusion.7
  53.1 0.0 copy-done.1
  53.1 0.0 copy-done.2
  53.1 66.6 %collective-permute-done.2 = bf16[3,32,64,256]{3,2,1,0:T(8,128)(2,1)S(1)} collective-permute-done((bf16[3,32,64,256]{3,2,1,0:T(8,128)(2,1)S(1)}, bf16[3,32,64,256]{3,2,1,0:T(8,128)(2,1)S(1)}, u32[]{:S(2)}, u32[]{:S(2)}) %collective-permute-start.2) | collective-permute-done | bytes 3145760 | tf_op jit(solution)/shard_map/ppermute | solution.py:26
  119.7 0.0 collective-permute-done.3
  119.7 2.0 %fusion = f32[3,32,256,64]{2,3,1,0:T(8,128)S(1)} fusion(bf16[3,32,64,256]{3,2,1,0:T(8,128)(2,1)S(1)} %collective-permute-done.3, bf16[3,32,64,256]{3,2,1,0:T(8,128)(2,1)S(1)} %fusion.18, bf16[3,32,64,256]{3,2,1,0:T(8,128)(2,1)S(1)} %collective-permute-done.2, f32[64]{0:T(128)S(1)} %sqrt.64, s32[192]{0:T(256)S(1)} %iota_add_fusion.1), kind=kOutput, calls=%fused_computation | convolution fusion | flops 632426496 | bytes 15729664 | tf_op jit(solution)/shard_map/kj,csjy->csky/dot_general | solution.py:132
  121.7 9.7 %fusion.69 = (f32[3,256]{1,0:T(4,128)S(1)}, f32[3,32,64,256]{3,1,2,0:T(8,128)S(1)}) fusion(f32[32]{0:T(128)S(1)} %compare_select_fusion, f32[3,32,256,64]{2,3,1,0:T(8,128)S(1)} %fusion), kind=kOutput, calls=%fused_computation.112 | convolution fusion | flops 605559040 | bytes 12586112 | tf_op jit(solution)/shard_map/ts,csky->ctky/dot_general | solution.py:136
  131.4 0.0 copy-start
  131.4 0.9 multiply_reduce_fusion
  132.3 1.8 %copy-done = f32[3,32,64,256]{3,1,2,0:T(8,128)} copy-done((f32[3,32,64,256]{3,1,2,0:T(8,128)}, f32[3,32,64,256]{3,1,2,0:T(8,128)S(1)}, u32[]{:S(2)}) %copy-start) | copy-done | bytes 6291480
  134.1 24.9 %all-reduce = (f32[3,256]{1,0:T(4,128)S(1)}, f32[6,256]{1,0:T(8,128)S(1)}) all-reduce(f32[3,256]{1,0:T(4,128)S(1)} %get-tuple-element.45, f32[6,256]{1,0:T(8,128)S(1)} %stack.33), channel_id=1, replica_groups=mesh['wall'=4,'span'=8] {'span'}, use_global_device_ids=true, to_apply=%region_10.11 | all-reduce | flops 2304 | bytes 18432 | tf_op jit(solution)/shard_map/psum | solution.py:160
  159.1 0.0 copy-start.3
  159.1 3.6 %broadcast_subtract_fusion = f32[3,32,64,256]{3,1,2,0:T(8,128)S(1)} fusion(f32[3,32,64,256]{3,1,2,0:T(8,128)} %copy-done, f32[3,256]{1,0:T(4,128)S(1)} %broadcast_multiply_fusion.1), kind=kLoop, calls=%fused_computation.17 | loop fusion | flops 1572864 | bytes 12585984 | tf_op jit(solution)/shard_map/sub | solution.py:100
  162.6 0.0 copy-done.3
  162.7 1.5 multiply_add_fusion.1
  164.3 1.1 pad_maximum_fusion
  165.4 6.4 %copy.7 = f32[3,32,64,256]{3,2,1,0:T(8,128)} copy(f32[3,32,64,256]{3,1,2,0:T(8,128)S(1)} %pad_maximum_fusion) | data formatting | bytes 12582912 | tf_op jit(solution)/shard_map/stack | solution.py:113
  (15 shorter events, 0.1 us)
Async XLA Ops:
  3.9 7.3 %copy-start.4 = (s32[256]{0:T(256)S(1)}, s32[256]{0:T(256)}, u32[]{:S(2)}) copy-start(s32[256]{0:T(256)} %param.6) | copy-start | bytes 3076
  4.9 38.6 %collective-permute-start = (bf16[3,32,64,128]{3,2,1,0:T(8,128)(2,1)S(1)}, bf16[3,32,64,128]{3,2,1,0:T(8,128)(2,1)S(1)}, u32[]{:S(2)}, u32[]{:S(2)}) collective-permute-start(bf16[3,32,64,128]{3,2,1,0:T(8,128)(2,1)S(1)} %get-tuple-element.20), channel_id=1, source_target_pairs={{0,8},{8,16},{16,24},{1,9},{9,17},{17,25},{2,10},{10,18},{18,26},{... | collective-permute-start | bytes 4718600 | tf_op jit(solution)/shard_map/ppermute | solution.py:26
  10.0 37.7 %collective-permute-start.1 = (bf16[3,32,64,128]{3,2,1,0:T(8,128)(2,1)S(1)}, bf16[3,32,64,128]{3,2,1,0:T(8,128)(2,1)S(1)}, u32[]{:S(2)}, u32[]{:S(2)}) collective-permute-start(bf16[3,32,64,128]{3,2,1,0:T(8,128)(2,1)S(1)} %get-tuple-element.21), channel_id=1, source_target_pairs={{8,0},{16,8},{24,16},{9,1},{17,9},{25,17},{10,2},{18,10},{26,18},{... | collective-permute-start | bytes 4718600 | tf_op jit(solution)/shard_map/ppermute | solution.py:28
  11.7 41.4 %copy-start.1 = (f32[3,256]{1,0:T(4,128)S(1)}, f32[3,256]{1,0:T(4,128)}, u32[]{:S(2)}) copy-start(f32[3,256]{1,0:T(4,128)} %param.9) | copy-start | bytes 9220
  11.7 41.4 %copy-start.2 = (f32[3,256]{1,0:T(4,128)S(1)}, f32[3,256]{1,0:T(4,128)}, u32[]{:S(2)}) copy-start(f32[3,256]{1,0:T(4,128)} %param.7) | copy-start | bytes 9220
  50.2 69.5 %collective-permute-start.2 = (bf16[3,32,64,256]{3,2,1,0:T(8,128)(2,1)S(1)}, bf16[3,32,64,256]{3,2,1,0:T(8,128)(2,1)S(1)}, u32[]{:S(2)}, u32[]{:S(2)}) collective-permute-start(bf16[3,32,64,256]{3,2,1,0:T(8,128)(2,1)S(1)} %fusion.18), channel_id=1, source_target_pairs={{0,1},{1,2},{2,3},{3,4},{4,5},{5,6},{6,7},{7,0},{8,9},{9,10},{10,1... | collective-permute-start | bytes 9437192 | tf_op jit(solution)/shard_map/ppermute | solution.py:26
  50.3 69.4 %collective-permute-start.3 = (bf16[3,32,64,256]{3,2,1,0:T(8,128)(2,1)S(1)}, bf16[3,32,64,256]{3,2,1,0:T(8,128)(2,1)S(1)}, u32[]{:S(2)}, u32[]{:S(2)}) collective-permute-start(bf16[3,32,64,256]{3,2,1,0:T(8,128)(2,1)S(1)} %fusion.18), channel_id=1, source_target_pairs={{1,0},{2,1},{3,2},{4,3},{5,4},{6,5},{7,6},{0,7},{9,8},{10,9},{11,1... | collective-permute-start | bytes 9437192 | tf_op jit(solution)/shard_map/ppermute | solution.py:28
  131.4 2.7 %copy-start = (f32[3,32,64,256]{3,1,2,0:T(8,128)}, f32[3,32,64,256]{3,1,2,0:T(8,128)S(1)}, u32[]{:S(2)}) copy-start(f32[3,32,64,256]{3,1,2,0:T(8,128)S(1)} %get-tuple-element.46) | copy-start | bytes 18874372
  159.1 3.6 %copy-start.3 = (f32[3,256]{1,0:T(4,128)S(1)}, f32[3,256]{1,0:T(4,128)}, u32[]{:S(2)}) copy-start(f32[3,256]{1,0:T(4,128)} %param.8) | copy-start | bytes 9220
where the time goes:
time: 172 us
  waiting for transfers between devices  103 us (60%)
  blocking collectives  24.9 us (14%)
  matrix products  14.2 us (8%)
  other arithmetic  11.6 us (7%)
  local copies, waits for them, and re-layouts  9.19 us (5%)
  starting transfers between devices  9.04 us (5%)
    ppermute x2, waiting for transfers between devices, padded_2(): lax.ppermute(tail, axis, [(i, (i + 1) % count) for i in range(ends)])  98.4 us
    psum x1, blocking collectives, shards(): lax.psum((local_sums, pair_sums(fluctuation)), 'span')  24.9 us
    dot_general x1, matrix products, time_filter(): jnp.einsum('ts,csky->ctky', memory, spanned, precision=lax.Precision.HIGH...  9.7 us
    another operation x1, local copies, waits for them, and re-layouts, rescaled_inflow(): return jnp.stack([first_component, second_component, third_component])  6.35 us
    ppermute x2, starting transfers between devices, padded_2(): lax.ppermute(tail, axis, [(i, (i + 1) % count) for i in range(ends)])  5.11 us
    ppermute x2, waiting for transfers between devices, padded_2(): lax.ppermute(head, axis, [((i + 1) % count, i) for i in range(ends)])  4.22 us
    convert_element_type x1, other arithmetic, to_field(): return (math.sqrt(12.0) * scaled).astype(jnp.bfloat16)  3.94 us
    ppermute x2, starting transfers between devices, padded_2(): lax.ppermute(head, axis, [((i + 1) % count, i) for i in range(ends)])  3.92 us
  transfers between devices with their start and end apart: 4, of which 3 were waited for; matrix products, arithmetic and copies ran while one was open for 0% of the time, Pallas kernels for 0%

commit v1 on v0

v1 whole, which is shorter than its diff:
```python
import functools
import math

import jax
import jax.numpy as jnp
from jax import lax
from jax.experimental import pallas as pl
from jax.experimental.pallas import tpu as pltpu
from jax.sharding import PartitionSpec as P

WMAX = 64
SPANW = 32
TSCALE = 8


PAIRS = ((0, 0), (1, 0), (1, 1), (2, 0), (2, 1), (2, 2))
SPREAD_FLOOR = 0.25
INV_RANGE = 1.0 / 1073741824.0


def to_field(noise_bits):
    scaled = (noise_bits.astype(jnp.float32) + 0.5) * INV_RANGE - 0.5
    return (math.sqrt(12.0) * scaled).astype(jnp.bfloat16)


def lund_transform(sample_covariance, target_factor_diagonal, target_factor_lower):
    cov_00 = sample_covariance[0] + SPREAD_FLOOR
    cov_10 = sample_covariance[1]
    cov_11 = sample_covariance[2] + SPREAD_FLOOR
    cov_20 = sample_covariance[3]
    cov_21 = sample_covariance[4]
    cov_22 = sample_covariance[5] + SPREAD_FLOOR
    chol_00 = jnp.sqrt(cov_00)
    chol_10 = cov_10 / chol_00
    chol_20 = cov_20 / chol_00
    chol_11 = jnp.sqrt(cov_11 - chol_10 * chol_10)
    chol_21 = (cov_21 - chol_20 * chol_10) / chol_11
    chol_22 = jnp.sqrt(cov_22 - chol_20 * chol_20 - chol_21 * chol_21)
    inv_00 = 1.0 / chol_00
    inv_11 = 1.0 / chol_11
    inv_22 = 1.0 / chol_22
    inv_10 = -chol_10 * inv_00 * inv_11
    inv_21 = -chol_21 * inv_11 * inv_22
    inv_20 = -(chol_20 * inv_00 + chol_21 * inv_10) * inv_22
    gain_00 = target_factor_diagonal[0] * inv_00
    gain_10 = target_factor_lower[0] * inv_00 + target_factor_diagonal[1] * inv_10
    gain_11 = target_factor_diagonal[1] * inv_11
    gain_20 = (
        target_factor_lower[1] * inv_00
        + target_factor_lower[2] * inv_10
        + target_factor_diagonal[2] * inv_20
    )
    gain_21 = target_factor_lower[2] * inv_11 + target_factor_diagonal[2] * inv_21
    gain_22 = target_factor_diagonal[2] * inv_22
    return gain_00, gain_10, gain_11, gain_20, gain_21, gain_22


CHUNK = 2
AHEAD = 4
BLOCK = 4
MESH = pl.DeviceIdType.MESH


def band_taps(offsets, spread, axis):
    inside = jnp.abs(offsets) <= 2.0 * spread
    safe_off = jnp.where(inside, offsets, 0.0)
    kernel = jnp.where(
        inside, jnp.exp(-math.pi * safe_off * safe_off / (8.0 * spread * spread)), 0.0
    )
    norm_total = jnp.sqrt(jnp.sum(kernel * kernel, axis=axis, keepdims=True))
    return (kernel / norm_total).astype(jnp.bfloat16)


def offsets_of(shape, in_axis, margin):
    return (
        lax.broadcasted_iota(jnp.int32, shape, in_axis)
        - margin
        - lax.broadcasted_iota(jnp.int32, shape, 1 - in_axis)
    ).astype(jnp.float32)


def filter_kernel(
    n_wall,
    n_span,
    noise_ref,
    widths_ref,
    fluct_ref,
    total_ref,
    stage,
    pad,
    wide,
    wall_band,
    span_band,
    last,
    moments,
    gather,
    noise_sem,
    wall_send,
    wall_recv,
    span_send,
    span_recv,
    sum_send,
    sum_recv,
):
    chunks, n_comp, chunk, n_cols, width = pad.shape
    n_rows = widths_ref.shape[1]
    margin = (width - n_rows) // 2
    span_margin = (wide.shape[3] - n_cols) // 2
    wall = lax.axis_index("wall")
    span = lax.axis_index("span")
    after = lax.rem(span + 1, n_span)
    before = lax.rem(span + n_span - 1, n_span)
    low = wall > 0
    high = wall < n_wall - 1

    def noise_copy(i):
        return pltpu.make_async_copy(
            noise_ref.at[:, pl.ds(i * chunk, chunk)], stage.at[i], noise_sem.at[i]
        )

    def to_lower(i):
        return pltpu.make_async_remote_copy(
            src_ref=pad.at[i, :, :, :, pl.ds(margin, margin)],
            dst_ref=pad.at[i, :, :, :, pl.ds(margin + n_rows, margin)],
            send_sem=wall_send.at[0, i],
            recv_sem=wall_recv.at[0, i],
            device_id={"wall": wall - 1},
            device_id_type=MESH,
        )

    def to_upper(i):
        return pltpu.make_async_remote_copy(
            src_ref=pad.at[i, :, :, :, pl.ds(n_rows, margin)],
            dst_ref=pad.at[i, :, :, :, pl.ds(0, margin)],
            send_sem=wall_send.at[1, i],
            recv_sem=wall_recv.at[1, i],
            device_id={"wall": wall + 1},
            device_id_type=MESH,
        )

    def to_before(i):
        return pltpu.make_async_remote_copy(
            src_ref=wide.at[i, :, :, pl.ds(span_margin, span_margin)],
            dst_ref=wide.at[i, :, :, pl.ds(span_margin + n_cols, span_margin)],
            send_sem=span_send.at[0, i],
            recv_sem=span_recv.at[0, i],
            device_id={"span": before},
            device_id_type=MESH,
        )

    def to_after(i):
        return pltpu.make_async_remote_copy(
            src_ref=wide.at[i, :, :, pl.ds(n_cols, span_margin)],
            dst_ref=wide.at[i, :, :, pl.ds(0, span_margin)],
            send_sem=span_send.at[1, i],
            recv_sem=span_recv.at[1, i],
            device_id={"span": after},
            device_id_type=MESH,
        )

    def sum_copy(k):
        return pltpu.make_async_remote_copy(
            src_ref=gather.at[span],
            dst_ref=gather.at[span],
            send_sem=sum_send.at[k],
            recv_sem=sum_recv.at[span],
            device_id={"span": lax.rem(span + k, n_span)},
            device_id_type=MESH,
        )

    barrier = pltpu.get_barrier_semaphore()
    for k in range(1, n_span):
        pl.semaphore_signal(
            barrier, inc=1, device_id={"span": lax.rem(span + k, n_span)}, device_id_type=MESH
        )

    @pl.when(low)
    def _():
        pl.semaphore_signal(barrier, inc=1, device_id={"wall": wall - 1}, device_id_type=MESH)

    @pl.when(high)
    def _():
        pl.semaphore_signal(barrier, inc=1, device_id={"wall": wall + 1}, device_id_type=MESH)

    @pl.loop(0, chunks)
    def _(i):
        noise_copy(i).start()

    def convert(i):
        noise_copy(i).wait()
        for c in range(n_comp):
            for s in range(chunk):
                pad[i, c, s, :, margin : margin + n_rows] = to_field(stage[i, c, s])

    def send_walls(i):
        @pl.when(low)
        def _():
            to_lower(i).start()

        @pl.when(high)
        def _():
            to_upper(i).start()

    convert(0)
    pl.semaphore_wait(
        barrier, n_span - 1 + low.astype(jnp.int32) + high.astype(jnp.int32)
    )
    send_walls(0)

    @pl.loop(1, min(AHEAD, chunks))
    def _(i):
        convert(i)
        send_walls(i)

    wall_band[...] = band_taps(
        offsets_of((width, n_rows), 0, margin), widths_ref[...].astype(jnp.float32), 0
    )
    span_band[...] = band_taps(
        offsets_of((n_cols, n_cols + 2 * span_margin), 1, span_margin),
        jnp.full((n_cols, 1), float(SPANW), jnp.float32),
        1,
    )

    @pl.when(jnp.logical_not(low))
    def _():
        @pl.loop(0, chunks)
        def _(i):
            pad[i, :, :, :, 0:margin] = jnp.zeros((n_comp, chunk, n_cols, margin), jnp.bfloat16)

    @pl.when(jnp.logical_not(high))
    def _():
        @pl.loop(0, chunks)
        def _(i):
            pad[i, :, :, :, margin + n_rows : width] = jnp.zeros(
                (n_comp, chunk, n_cols, margin), jnp.bfloat16
            )

    @pl.loop(0, chunks)
    def _(i):
        @pl.when(low)
        def _():
            to_upper(i).wait_recv()

        @pl.when(high)
        def _():
            to_lower(i).wait_recv()

        window = pad[i].reshape(n_comp * chunk * n_cols, width)
        smooth = jnp.dot(window, wall_band[...], preferred_element_type=jnp.float32)
        wide[i, :, :, span_margin : span_margin + n_cols] = smooth.astype(jnp.bfloat16).reshape(
            n_comp, chunk, n_cols, n_rows
        )
        to_before(i).start()
        to_after(i).start()

        @pl.when(i + AHEAD < chunks)
        def _():
            convert(i + AHEAD)
            send_walls(i + AHEAD)

    decay = math.exp(-math.pi / (2.0 * TSCALE))
    fresh = math.sqrt(1.0 - decay * decay)
    last[...] = jnp.zeros_like(last)
    moments[...] = jnp.zeros_like(moments)

    def fold(values):
        return jnp.sum(values.reshape(n_cols // 8, 8, n_rows), axis=0)

    @pl.loop(0, chunks)
    def _(i):
        to_before(i).wait_recv()
        to_after(i).wait_recv()
        for s in range(chunk):
            gain = jnp.where(i * chunk + s == 0, 1.0, fresh).astype(jnp.float32)
            now = []
            for c in range(n_comp):
                spanned = jnp.dot(
                    span_band[...], wide[i, c, s], preferred_element_type=jnp.float32
                )
                value = decay * last[c] + gain * spanned
                last[c] = value
                fluct_ref[c, i * chunk + s] = value
                now.append(value)
            for c in range(n_comp):
                moments[c] += fold(now[c])
            for slot, (one, two) in enumerate(PAIRS):
                moments[n_comp + slot] += fold(now[one] * now[two])

    gather[span] = jnp.sum(moments[...], axis=1)
    for k in range(1, n_span):
        sum_copy(k).start()

    @pl.loop(0, chunks)
    def _(i):
        @pl.when(low)
        def _():
            to_lower(i).wait_send()

        @pl.when(high)
        def _():
            to_upper(i).wait_send()

        to_before(i).wait_send()
        to_after(i).wait_send()

    for k in range(1, n_span):
        source = lax.rem(span + k, n_span)
        pltpu.make_async_remote_copy(
            src_ref=gather.at[span],
            dst_ref=gather.at[source],
            send_sem=sum_send.at[k],
            recv_sem=sum_recv.at[source],
            device_id={"span": source},
            device_id_type=MESH,
        ).wait_recv()
    total = gather[0]
    for k in range(1, n_span):
        total = total + gather[k]
    total_ref[...] = total
    for k in range(1, n_span):
        sum_copy(k).wait_send()


def scale_kernel(cell_count, fluct_ref, total_ref, mean_ref, diag_ref, lower_ref, out_ref, rows):
    @pl.when(pl.program_id(0) == 0)
    def _():
        means = [total_ref[c : c + 1] / cell_count for c in range(3)]
        spread = [
            total_ref[3 + slot : 4 + slot] / cell_count - means[one] * means[two]
            for slot, (one, two) in enumerate(PAIRS)
        ]
        gains = lund_transform(
            spread,
            [diag_ref[c : c + 1] for c in range(3)],
            [lower_ref[c : c + 1] for c in range(3)],
        )
        for slot, row in enumerate(means + list(gains)):
            rows[slot : slot + 1] = row

    row = [rows[slot : slot + 1] for slot in range(9)]
    mean = [mean_ref[c : c + 1] for c in range(3)]
    first = pl.program_id(0) * out_ref.shape[1]
    for s in range(out_ref.shape[1]):
        centred = [fluct_ref[c, first + s] - row[c] for c in range(3)]
        out_ref[0, s] = mean[0] + row[3] * centred[0]
        out_ref[1, s] = mean[1] + row[4] * centred[0] + row[5] * centred[1]
        out_ref[2, s] = mean[2] + row[6] * centred[0] + row[7] * centred[1] + row[8] * centred[2]


def shards(
    noise_bits, filter_widths, target_mean_profile, target_factor_diagonal, target_factor_lower
):
    n_comp, n_samples, n_cols, n_rows = noise_bits.shape
    n_wall, n_span = lax.axis_size("wall"), lax.axis_size("span")
    margin = 2 * WMAX
    span_margin = 2 * SPANW
    chunks = n_samples // CHUNK
    n_sums = n_comp + len(PAIRS)
    vmem = pl.BlockSpec(memory_space=pltpu.VMEM)
    fluct, total = pl.pallas_call(
        functools.partial(filter_kernel, n_wall, n_span),
        out_shape=[
            pltpu.VMEM(noise_bits.shape, jnp.float32),
            pltpu.VMEM((n_sums, n_rows), jnp.float32),
        ],
        in_specs=[pl.BlockSpec(memory_space=pl.ANY), vmem],
        out_specs=[vmem, vmem],
        scratch_shapes=[
            pltpu.VMEM((chunks, n_comp, CHUNK, n_cols, n_rows), jnp.int32),
            pltpu.VMEM((chunks, n_comp, CHUNK, n_cols, n_rows + 2 * margin), jnp.bfloat16),
            pltpu.VMEM((chunks, n_comp, CHUNK, n_cols + 2 * span_margin, n_rows), jnp.bfloat16),
            pltpu.VMEM((n_rows + 2 * margin, n_rows), jnp.bfloat16),
            pltpu.VMEM((n_cols, n_cols + 2 * span_margin), jnp.bfloat16),
            pltpu.VMEM((n_comp, n_cols, n_rows), jnp.float32),
            pltpu.VMEM((n_sums, 8, n_rows), jnp.float32),
            pltpu.VMEM((n_span, n_sums, n_rows), jnp.float32),
            pltpu.SemaphoreType.DMA((chunks,)),
            pltpu.SemaphoreType.DMA((2, chunks)),
            pltpu.SemaphoreType.DMA((2, chunks)),
            pltpu.SemaphoreType.DMA((2, chunks)),
            pltpu.SemaphoreType.DMA((2, chunks)),
            pltpu.SemaphoreType.DMA((n_span,)),
            pltpu.SemaphoreType.DMA((n_span,)),
        ],
        compiler_params=pltpu.CompilerParams(
            collective_id=0, has_side_effects=True, vmem_limit_bytes=54 * 1024 * 1024
        ),
        name="filters",
    )(noise_bits, filter_widths.reshape(1, n_rows))
    block = (n_comp, BLOCK, n_cols, n_rows)
    return pl.pallas_call(
        functools.partial(scale_kernel, float(n_samples * n_cols * n_span)),
        out_shape=jax.ShapeDtypeStruct(noise_bits.shape, jnp.float32),
        grid=(n_samples // BLOCK,),
        in_specs=[vmem, vmem, vmem, vmem, vmem],
        out_specs=pl.BlockSpec(block, lambda i: (0, i, 0, 0)),
        scratch_shapes=[pltpu.VMEM((9, n_rows), jnp.float32)],
        compiler_params=pltpu.CompilerParams(vmem_limit_bytes=16 * 1024 * 1024),
        name="rescale",
    )(fluct, total, target_mean_profile, target_factor_diagonal, target_factor_lower)


def solution(mesh):
    placed = (
        P(None, None, "span", "wall"),
        P("wall"),
        P(None, "wall"),
        P(None, "wall"),
        P(None, "wall"),
    )
    return jax.shard_map(
        shards, mesh=mesh, in_specs=placed, out_specs=P(None, None, "span", "wall"), check_vma=False
    )
```

time: 172 us -> 87.5 us (0.51)
  waiting for transfers between devices: 103 us -> 0 us
  Pallas kernels: 0 us -> 87.3 us
  blocking collectives: 24.9 us -> 0 us
  matrix products: 14.2 us -> 0 us
  other arithmetic: 11.6 us -> 0 us
  local copies, waits for them, and re-layouts: 9.19 us -> 0.01 us
  starting transfers between devices: 9.04 us -> 0 us
    ppermute x4 -> x0, waiting for transfers between devices: 103 us -> none  [the longest x2 98.4 us: padded_2(): lax.ppermute(tail, axis, [(i, (i + 1) % count) for i in range(ends)])]
    pallas_call x0 -> x2, Pallas kernels: none -> 87.3 us  [the longest x1 82.8 us: shards(): pl.pallas_call(functools.partial(filter_kernel, n_wall, n_span), out_shap...]
    psum x1 -> x0, blocking collectives: 24.9 us -> none  [shards(): lax.psum((local_sums, pair_sums(fluctuation)), 'span')]
    dot_general x3 -> x0, matrix products: 14.2 us -> none  [the longest x1 9.7 us: time_filter(): jnp.einsum('ts,csky->ctky', memory, spanned, precision=lax.Precision.HIGH...]
    ppermute x4 -> x0, starting transfers between devices: 9.04 us -> none  [the longest x2 5.11 us: padded_2(): lax.ppermute(tail, axis, [(i, (i + 1) % count) for i in range(ends)])]
    another operation x2 -> x0, local copies, waits for them, and re-layouts: 6.38 us -> none  [the longest x1 6.35 us: rescaled_inflow(): return jnp.stack([first_component, second_component, third_component])]
    convert_element_type x1 -> x0, other arithmetic: 3.94 us -> none  [to_field(): return (math.sqrt(12.0) * scaled).astype(jnp.bfloat16)]
    sub x3 -> x0, other arithmetic: 3.56 us -> none  [the longest x1 3.56 us: rescaled_inflow(): centred_samples = fluctuation - per_row_means[:, None, None, :]]
  transfers between devices with their start and end apart: 4 -> 0, of which waited for: 3 -> 0; matrix products, arithmetic and copies ran while one was open for 0% -> 0% of each run, Pallas kernels for 0% -> 0%
where the time goes in v1:
time: 87.5 us; the launch traced here: 87.3 us
  Pallas kernels  87.3 us (100%)
    pallas_call x1, Pallas kernels, shards(): pl.pallas_call(functools.partial(filter_kernel, n_wall, n_span), out_shap...  82.8 us
    pallas_call x1, Pallas kernels, shards(): pl.pallas_call(functools.partial(scale_kernel, float(n_samples * n_cols *...  4.44 us

profile of v1, /device:TPU:0, one launch (start us, length us, event | category | flops | bytes accessed | tf_op | source)
XLA Modules:
  0.0 87.3 jit_solution(2420359244692113832)
XLA Ops:
  0.0 0.0 copy-start.2
  0.0 0.0 copy-start.1
  0.0 0.0 copy-start
  0.0 82.8 %filters.1 = (f32[3,32,64,256]{3,2,1,0:T(8,128)S(1)}, f32[9,256]{1,0:T(8,128)S(1)}) custom-call(s32[3,32,64,256]{3,2,1,0:T(8,128)} %noise_ref.1, s32[1,256]{1,0:T(1,128)} %bitcast.1), custom_call_target="tpu_custom_call" | custom-call | tf_op jit(solution)/shard_map/filters/pallas_call | solution.py:360
  82.9 0.0 copy-done.2
  82.9 0.0 copy-done.1
  82.9 0.0 copy-done
  82.9 4.4 %rescale.1 = f32[3,32,64,256]{3,2,1,0:T(8,128)} custom-call(f32[3,32,64,256]{3,2,1,0:T(8,128)S(1)} %get-tuple-element.7.fluct_ref, f32[9,256]{1,0:T(8,128)S(1)} %get-tuple-element.8.total_ref, f32[3,256]{1,0:T(4,128)S(1)} %copy-done, f32[3,256]{1,0:T(4,128)S(1)} %copy-done.1, f32[3,256]{1,0:T(4,128)S(1)} %copy-done.2), custom_call_target="tpu_custom_call" | custom-call | tf_op jit(solution)/shard_map/rescale/pallas_call | solution.py:391
Async XLA Ops:
  0.0 82.9 %copy-start.2 = (f32[3,256]{1,0:T(4,128)S(1)}, f32[3,256]{1,0:T(4,128)}, u32[]{:S(2)}) copy-start(f32[3,256]{1,0:T(4,128)} %lower_ref.1) | copy-start | bytes 9220
  0.0 82.9 %copy-start.1 = (f32[3,256]{1,0:T(4,128)S(1)}, f32[3,256]{1,0:T(4,128)}, u32[]{:S(2)}) copy-start(f32[3,256]{1,0:T(4,128)} %diag_ref.1) | copy-start | bytes 9220
  0.0 82.9 %copy-start = (f32[3,256]{1,0:T(4,128)S(1)}, f32[3,256]{1,0:T(4,128)}, u32[]{:S(2)}) copy-start(f32[3,256]{1,0:T(4,128)} %mean_ref.1) | copy-start | bytes 9220

commit v2 on v1

--- a/solution.py
+++ b/solution.py
@@ -55,9 +55,10 @@
     return gain_00, gain_10, gain_11, gain_20, gain_21, gain_22
 
 
-CHUNK = 2
-AHEAD = 4
-BLOCK = 4
+CHUNK = 1
+EARLY = 2
+AHEAD = 6
+BLOCK = 2
 MESH = pl.DeviceIdType.MESH
 
 
@@ -86,6 +87,7 @@
     widths_ref,
     fluct_ref,
     total_ref,
+    widths_vmem,
     stage,
     pad,
     wide,
@@ -94,6 +96,7 @@
     last,
     moments,
     gather,
+    widths_sem,
     noise_sem,
     wall_send,
     wall_recv,
@@ -168,6 +171,10 @@
             device_id_type=MESH,
         )
 
+    early = min(EARLY, chunks - 1)
+    ready = min(early + AHEAD, chunks)
+    for i in range(early):
+        noise_copy(i).start()
     barrier = pltpu.get_barrier_semaphore()
     for k in range(1, n_span):
         pl.semaphore_signal(
@@ -182,9 +189,10 @@
     def _():
         pl.semaphore_signal(barrier, inc=1, device_id={"wall": wall + 1}, device_id_type=MESH)
 
-    @pl.loop(0, chunks)
-    def _(i):
+    widths_copy = pltpu.make_async_copy(widths_ref, widths_vmem, widths_sem)
+    for i in range(early, early + 2):
         noise_copy(i).start()
+    widths_copy.start()
 
     def convert(i):
         noise_copy(i).wait()
@@ -192,6 +200,12 @@
             for s in range(chunk):
                 pad[i, c, s, :, margin : margin + n_rows] = to_field(stage[i, c, s])
 
+    def convert_early(i):
+        noise_copy(i).wait()
+        for c in range(n_comp):
+            for s in range(chunk):
+                wide[i, c, s, span_margin : span_margin + n_cols] = to_field(stage[i, c, s])
+
     def send_walls(i):
         @pl.when(low)
         def _():
@@ -201,19 +215,29 @@
         def _():
             to_upper(i).start()
 
-    convert(0)
+    convert_early(0)
     pl.semaphore_wait(
         barrier, n_span - 1 + low.astype(jnp.int32) + high.astype(jnp.int32)
     )
-    send_walls(0)
-
-    @pl.loop(1, min(AHEAD, chunks))
+    to_before(0).start()
+    to_after(0).start()
+    for i in range(1, early):
+        convert_early(i)
+        to_before(i).start()
+        to_after(i).start()
+
+    @pl.loop(early + 2, chunks)
+    def _(i):
+        noise_copy(i).start()
+
+    @pl.loop(early, ready)
     def _(i):
         convert(i)
         send_walls(i)
 
+    widths_copy.wait()
     wall_band[...] = band_taps(
-        offsets_of((width, n_rows), 0, margin), widths_ref[...].astype(jnp.float32), 0
+        offsets_of((width, n_rows), 0, margin), widths_vmem[...].astype(jnp.float32), 0
     )
     span_band[...] = band_taps(
         offsets_of((n_cols, n_cols + 2 * span_margin), 1, span_margin),
@@ -235,8 +259,7 @@
                 (n_comp, chunk, n_cols, margin), jnp.bfloat16
             )
 
-    @pl.loop(0, chunks)
-    def _(i):
+    def wait_walls(i):
         @pl.when(low)
         def _():
             to_upper(i).wait_recv()
@@ -245,18 +268,35 @@
         def _():
             to_lower(i).wait_recv()
 
+    def wall_filter(i):
         window = pad[i].reshape(n_comp * chunk * n_cols, width)
         smooth = jnp.dot(window, wall_band[...], preferred_element_type=jnp.float32)
-        wide[i, :, :, span_margin : span_margin + n_cols] = smooth.astype(jnp.bfloat16).reshape(
-            n_comp, chunk, n_cols, n_rows
-        )
+        return smooth.reshape(n_comp, chunk, n_cols, n_rows)
+
+    def span_filter(i, c, s):
+        return jnp.dot(span_band[...], wide[i, c, s], preferred_element_type=jnp.float32)
+
+    @pl.loop(early, chunks)
+    def _(i):
+        wait_walls(i)
+        wide[i, :, :, span_margin : span_margin + n_cols] = wall_filter(i).astype(jnp.bfloat16)
         to_before(i).start()
         to_after(i).start()
 
-        @pl.when(i + AHEAD < chunks)
-        def _():
-            convert(i + AHEAD)
-            send_walls(i + AHEAD)
+        @pl.when(i + ready - early < chunks)
+        def _():
+            convert(i + ready - early)
+            send_walls(i + ready - early)
+
+    for i in range(early):
+        to_before(i).wait_recv()
+        to_after(i).wait_recv()
+        for c in range(n_comp):
+            for s in range(chunk):
+                pad[i, c, s, :, margin : margin + n_rows] = span_filter(i, c, s).astype(
+                    jnp.bfloat16
+                )
+        send_walls(i)
 
     decay = math.exp(-math.pi / (2.0 * TSCALE))
     fresh = math.sqrt(1.0 - decay * decay)
@@ -266,25 +306,31 @@
     def fold(values):
         return jnp.sum(values.reshape(n_cols // 8, 8, n_rows), axis=0)
 
-    @pl.loop(0, chunks)
+    def advance(time, spanned):
+        gain = jnp.where(time == 0, 1.0, fresh).astype(jnp.float32)
+        now = []
+        for c in range(n_comp):
+            value = decay * last[c] + gain * spanned(c)
+            last[c] = value
+            fluct_ref[c, time] = value
+            now.append(value)
+        for c in range(n_comp):
+            moments[c] += fold(now[c])
+        for slot, (one, two) in enumerate(PAIRS):
+            moments[n_comp + slot] += fold(now[one] * now[two])
+
+    for i in range(early):
+        wait_walls(i)
+        filtered = wall_filter(i)
+        for s in range(chunk):
+            advance(i * chunk + s, lambda c: filtered[c, s])
+
+    @pl.loop(early, chunks)
     def _(i):
         to_before(i).wait_recv()
         to_after(i).wait_recv()
         for s in range(chunk):
-            gain = jnp.where(i * chunk + s == 0, 1.0, fresh).astype(jnp.float32)
-            now = []
-            for c in range(n_comp):
-                spanned = jnp.dot(
-                    span_band[...], wide[i, c, s], preferred_element_type=jnp.float32
-                )
-                value = decay * last[c] + gain * spanned
-                last[c] = value
-                fluct_ref[c, i * chunk + s] = value
-                now.append(value)
-            for c in range(n_comp):
-                moments[c] += fold(now[c])
-            for slot, (one, two) in enumerate(PAIRS):
-                moments[n_comp + slot] += fold(now[one] * now[two])
+            advance(i * chunk + s, lambda c: span_filter(i, c, s))
 
     gather[span] = jnp.sum(moments[...], axis=1)
     for k in range(1, n_span):
@@ -321,30 +367,46 @@
         sum_copy(k).wait_send()
 
 
-def scale_kernel(cell_count, fluct_ref, total_ref, mean_ref, diag_ref, lower_ref, out_ref, rows):
-    @pl.when(pl.program_id(0) == 0)
-    def _():
-        means = [total_ref[c : c + 1] / cell_count for c in range(3)]
-        spread = [
-            total_ref[3 + slot : 4 + slot] / cell_count - means[one] * means[two]
-            for slot, (one, two) in enumerate(PAIRS)
-        ]
-        gains = lund_transform(
-            spread,
-            [diag_ref[c : c + 1] for c in range(3)],
-            [lower_ref[c : c + 1] for c in range(3)],
-        )
-        for slot, row in enumerate(means + list(gains)):
-            rows[slot : slot + 1] = row
-
-    row = [rows[slot : slot + 1] for slot in range(9)]
-    mean = [mean_ref[c : c + 1] for c in range(3)]
-    first = pl.program_id(0) * out_ref.shape[1]
-    for s in range(out_ref.shape[1]):
-        centred = [fluct_ref[c, first + s] - row[c] for c in range(3)]
-        out_ref[0, s] = mean[0] + row[3] * centred[0]
-        out_ref[1, s] = mean[1] + row[4] * centred[0] + row[5] * centred[1]
-        out_ref[2, s] = mean[2] + row[6] * centred[0] + row[7] * centred[1] + row[8] * centred[2]
+def scale_kernel(
+    cell_count, fluct_ref, total_ref, mean_ref, diag_ref, lower_ref, out_ref, scaled, out_sem
+):
+    n_rows = total_ref.shape[1]
+    blocks = scaled.shape[1] // BLOCK
+    means = [total_ref[c : c + 1] / cell_count for c in range(3)]
+    spread = [
+        total_ref[3 + slot : 4 + slot] / cell_count - means[one] * means[two]
+        for slot, (one, two) in enumerate(PAIRS)
+    ]
+    gains = lund_transform(
+        spread,
+        [diag_ref[c : c + 1] for c in range(3)],
+        [lower_ref[c : c + 1] for c in range(3)],
+    )
+    row = [jnp.broadcast_to(value, (8, n_rows)) for value in means + list(gains)]
+    mean = [jnp.broadcast_to(mean_ref[c : c + 1], (8, n_rows)) for c in range(3)]
+
+    def out_copy(i):
+        piece = pl.ds(i * BLOCK, BLOCK)
+        return pltpu.make_async_copy(scaled.at[:, piece], out_ref.at[:, piece], out_sem.at[i])
+
+    @pl.loop(0, blocks)
+    def _(i):
+        for s in range(BLOCK):
+            time = i * BLOCK + s
+            for j in range(0, scaled.shape[2], 8):
+                centred = [fluct_ref[c, time, j : j + 8] - row[c] for c in range(3)]
+                scaled[0, time, j : j + 8] = mean[0] + row[3] * centred[0]
+                scaled[1, time, j : j + 8] = (
+                    mean[1] + row[4] * centred[0] + row[5] * centred[1]
+                )
+                scaled[2, time, j : j + 8] = (
+                    mean[2] + row[6] * centred[0] + row[7] * centred[1] + row[8] * centred[2]
+                )
+        out_copy(i).start()
+
+    @pl.loop(0, blocks)
+    def _(i):
+        out_copy(i).wait()
 
 
 def shards(
@@ -363,9 +425,10 @@
             pltpu.VMEM(noise_bits.shape, jnp.float32),
             pltpu.VMEM((n_sums, n_rows), jnp.float32),
         ],
-        in_specs=[pl.BlockSpec(memory_space=pl.ANY), vmem],
+        in_specs=[pl.BlockSpec(memory_space=pl.ANY)] * 2,
         out_specs=[vmem, vmem],
         scratch_shapes=[
+            pltpu.VMEM((1, n_rows), jnp.int32),
             pltpu.VMEM((chunks, n_comp, CHUNK, n_cols, n_rows), jnp.int32),
             pltpu.VMEM((chunks, n_comp, CHUNK, n_cols, n_rows + 2 * margin), jnp.bfloat16),
             pltpu.VMEM((chunks, n_comp, CHUNK, n_cols + 2 * span_margin, n_rows), jnp.bfloat16),
@@ -374,6 +437,7 @@
             pltpu.VMEM((n_comp, n_cols, n_rows), jnp.float32),
             pltpu.VMEM((n_sums, 8, n_rows), jnp.float32),
             pltpu.VMEM((n_span, n_sums, n_rows), jnp.float32),
+            pltpu.SemaphoreType.DMA,
             pltpu.SemaphoreType.DMA((chunks,)),
             pltpu.SemaphoreType.DMA((2, chunks)),
             pltpu.SemaphoreType.DMA((2, chunks)),
@@ -387,14 +451,15 @@
         ),
         name="filters",
     )(noise_bits, filter_widths.reshape(1, n_rows))
-    block = (n_comp, BLOCK, n_cols, n_rows)
     return pl.pallas_call(
         functools.partial(scale_kernel, float(n_samples * n_cols * n_span)),
         out_shape=jax.ShapeDtypeStruct(noise_bits.shape, jnp.float32),
-        grid=(n_samples // BLOCK,),
-        in_specs=[vmem, vmem, vmem, vmem, vmem],
-        out_specs=pl.BlockSpec(block, lambda i: (0, i, 0, 0)),
-        scratch_shapes=[pltpu.VMEM((9, n_rows), jnp.float32)],
+        in_specs=[vmem] * 5,
+        out_specs=pl.BlockSpec(memory_space=pl.ANY),
+        scratch_shapes=[
+            pltpu.VMEM(noise_bits.shape, jnp.float32),
+            pltpu.SemaphoreType.DMA((n_samples // BLOCK,)),
+        ],
         compiler_params=pltpu.CompilerParams(vmem_limit_bytes=16 * 1024 * 1024),
         name="rescale",
     )(fluct, total, target_mean_profile, target_factor_diagonal, target_factor_lower)

time: 87.5 us -> 82.2 us (0.939)
  Pallas kernels: 87.3 us -> 82 us
    pallas_call x1, Pallas kernels: 82.8 us -> 79.1 us  [shards(): pl.pallas_call(functools.partial(filter_kernel, n_wall, n_span), out_shap...]
    pallas_call x1, Pallas kernels: 4.44 us -> 2.91 us  [shards(): pl.pallas_call(functools.partial(scale_kernel, float(n_samples * n_cols *...]
where the time goes in v2:
time: 82.2 us; the launch traced here: 82 us
  Pallas kernels  82 us (100%)
    pallas_call x1, Pallas kernels, shards(): pl.pallas_call(functools.partial(filter_kernel, n_wall, n_span), out_shap...  79.1 us
    pallas_call x1, Pallas kernels, shards(): pl.pallas_call(functools.partial(scale_kernel, float(n_samples * n_cols *...  2.91 us

profile of v2, /device:TPU:0, one launch (start us, length us, event | category | flops | bytes accessed | tf_op | source)
XLA Modules:
  0.0 82.0 jit_solution(8206160951312123899)
XLA Ops:
  0.0 0.0 copy-start.2
  0.0 0.0 copy-start.1
  0.0 0.0 copy-start
  0.0 79.1 %filters.1 = (f32[3,32,64,256]{3,2,1,0:T(8,128)S(1)}, f32[9,256]{1,0:T(8,128)S(1)}) custom-call(s32[3,32,64,256]{3,2,1,0:T(8,128)} %noise_ref.1, s32[1,256]{1,0:T(1,128)} %bitcast.1), custom_call_target="tpu_custom_call" | custom-call | tf_op jit(solution)/shard_map/filters/pallas_call | solution.py:422
  79.1 0.0 copy-done.2
  79.1 0.0 copy-done.1
  79.1 0.0 copy-done
  79.1 2.9 %rescale.1 = f32[3,32,64,256]{3,2,1,0:T(8,128)} custom-call(f32[3,32,64,256]{3,2,1,0:T(8,128)S(1)} %get-tuple-element.7.fluct_ref, f32[9,256]{1,0:T(8,128)S(1)} %get-tuple-element.8.total_ref, f32[3,256]{1,0:T(4,128)S(1)} %copy-done, f32[3,256]{1,0:T(4,128)S(1)} %copy-done.1, f32[3,256]{1,0:T(4,128)S(1)} %copy-done.2), custom_call_target="tpu_custom_call" | custom-call | tf_op jit(solution)/shard_map/rescale/pallas_call | solution.py:454
Async XLA Ops:
  0.0 79.1 %copy-start.2 = (f32[3,256]{1,0:T(4,128)S(1)}, f32[3,256]{1,0:T(4,128)}, u32[]{:S(2)}) copy-start(f32[3,256]{1,0:T(4,128)} %lower_ref.1) | copy-start | bytes 9220
  0.0 79.1 %copy-start.1 = (f32[3,256]{1,0:T(4,128)S(1)}, f32[3,256]{1,0:T(4,128)}, u32[]{:S(2)}) copy-start(f32[3,256]{1,0:T(4,128)} %diag_ref.1) | copy-start | bytes 9220
  0.0 79.1 %copy-start = (f32[3,256]{1,0:T(4,128)S(1)}, f32[3,256]{1,0:T(4,128)}, u32[]{:S(2)}) copy-start(f32[3,256]{1,0:T(4,128)} %mean_ref.1) | copy-start | bytes 9220

commit v3 on v2

--- a/solution.py
+++ b/solution.py
@@ -55,9 +55,9 @@
     return gain_00, gain_10, gain_11, gain_20, gain_21, gain_22
 
 
-CHUNK = 1
+CHUNK = 2
 EARLY = 2
-AHEAD = 6
+AHEAD = 3
 BLOCK = 2
 MESH = pl.DeviceIdType.MESH
 
@@ -332,7 +332,9 @@
         for s in range(chunk):
             advance(i * chunk + s, lambda c: span_filter(i, c, s))
 
-    gather[span] = jnp.sum(moments[...], axis=1)
+    sums = jnp.sum(moments[...], axis=1)
+    for slot in range(sums.shape[0]):
+        gather[span, :, slot * n_rows : (slot + 1) * n_rows] = sums[slot : slot + 1]
     for k in range(1, n_span):
         sum_copy(k).start()
 
@@ -362,7 +364,8 @@
     total = gather[0]
     for k in range(1, n_span):
         total = total + gather[k]
-    total_ref[...] = total
+    for slot in range(moments.shape[0]):
+        total_ref[slot : slot + 1] = total[:, slot * n_rows : (slot + 1) * n_rows]
     for k in range(1, n_span):
         sum_copy(k).wait_send()
 
@@ -436,7 +439,7 @@
             pltpu.VMEM((n_cols, n_cols + 2 * span_margin), jnp.bfloat16),
             pltpu.VMEM((n_comp, n_cols, n_rows), jnp.float32),
             pltpu.VMEM((n_sums, 8, n_rows), jnp.float32),
-            pltpu.VMEM((n_span, n_sums, n_rows), jnp.float32),
+            pltpu.VMEM((n_span, 1, n_sums * n_rows), jnp.float32),
             pltpu.SemaphoreType.DMA,
             pltpu.SemaphoreType.DMA((chunks,)),
             pltpu.SemaphoreType.DMA((2, chunks)),

time: 82.2 us -> 80.9 us (0.984)
  Pallas kernels: 82 us -> 80.7 us
    pallas_call x1, Pallas kernels: 79.1 us -> 77.8 us  [shards(): pl.pallas_call(functools.partial(filter_kernel, n_wall, n_span), out_shap...]
where the time goes in v3:
time: 80.9 us; the launch traced here: 80.7 us
  Pallas kernels  80.7 us (100%)
    pallas_call x1, Pallas kernels, shards(): pl.pallas_call(functools.partial(filter_kernel, n_wall, n_span), out_shap...  77.8 us
    pallas_call x1, Pallas kernels, shards(): pl.pallas_call(functools.partial(scale_kernel, float(n_samples * n_cols *...  2.91 us

profile of v3, /device:TPU:0, one launch (start us, length us, event | category | flops | bytes accessed | tf_op | source)
XLA Modules:
  0.0 80.7 jit_solution(14526876115433565723)
XLA Ops:
  0.0 0.0 copy-start.2
  0.0 0.0 copy-start.1
  0.0 0.0 copy-start
  0.0 77.8 %filters.1 = (f32[3,32,64,256]{3,2,1,0:T(8,128)S(1)}, f32[9,256]{1,0:T(8,128)S(1)}) custom-call(s32[3,32,64,256]{3,2,1,0:T(8,128)} %noise_ref.1, s32[1,256]{1,0:T(1,128)} %bitcast.1), custom_call_target="tpu_custom_call" | custom-call | tf_op jit(solution)/shard_map/filters/pallas_call | solution.py:425
  77.8 0.0 copy-done.2
  77.8 0.0 copy-done.1
  77.8 0.0 copy-done
  77.8 2.9 %rescale.1 = f32[3,32,64,256]{3,2,1,0:T(8,128)} custom-call(f32[3,32,64,256]{3,2,1,0:T(8,128)S(1)} %get-tuple-element.7.fluct_ref, f32[9,256]{1,0:T(8,128)S(1)} %get-tuple-element.8.total_ref, f32[3,256]{1,0:T(4,128)S(1)} %copy-done, f32[3,256]{1,0:T(4,128)S(1)} %copy-done.1, f32[3,256]{1,0:T(4,128)S(1)} %copy-done.2), custom_call_target="tpu_custom_call" | custom-call | tf_op jit(solution)/shard_map/rescale/pallas_call | solution.py:457
Async XLA Ops:
  0.0 77.8 %copy-start.2 = (f32[3,256]{1,0:T(4,128)S(1)}, f32[3,256]{1,0:T(4,128)}, u32[]{:S(2)}) copy-start(f32[3,256]{1,0:T(4,128)} %lower_ref.1) | copy-start | bytes 9220
  0.0 77.8 %copy-start.1 = (f32[3,256]{1,0:T(4,128)S(1)}, f32[3,256]{1,0:T(4,128)}, u32[]{:S(2)}) copy-start(f32[3,256]{1,0:T(4,128)} %diag_ref.1) | copy-start | bytes 9220
  0.0 77.8 %copy-start = (f32[3,256]{1,0:T(4,128)S(1)}, f32[3,256]{1,0:T(4,128)}, u32[]{:S(2)}) copy-start(f32[3,256]{1,0:T(4,128)} %mean_ref.1) | copy-start | bytes 9220
